TPU v7x, 32 devices: a 4x4x1 block of a 4x4x8 slice. The times are simulated.
32 devices in a mesh: dp: 1 (over z), tp: 4 (over y), cp: 8 (over x, core).
Axes of the slice: x: 4, y: 4, z: 1, core: 2. Of those that a mesh axis runs over, the one named last changes fastest.
The devices are a block of a 4x4x8 slice.
Arguments:
- hidden: bfloat16 [16, 64, 3072], P('dp')
- prefix_len: int32 [16], P('dp')
- k_cache: bfloat16 [16, 16384, 8, 128], P('dp', 'cp', 'tp')
- v_cache: bfloat16 [16, 16384, 8, 128], P('dp', 'cp', 'tp')
- attn_norm: bfloat16 [3072], replicated
- w_q: bfloat16 [3072, 3072], P(None, 'tp')
- w_k: bfloat16 [3072, 1024], P(None, 'tp')
- w_v: bfloat16 [3072, 1024], P(None, 'tp')
- w_o: bfloat16 [3072, 3072], P('tp')
- q_norm: bfloat16 [128], replicated
- k_norm: bfloat16 [128], replicated
Outputs:
- output 1: bfloat16 [16, 64, 3072], P('dp')
- output 2: bfloat16 [16, 64, 8, 128], P('dp', None, 'tp')
- output 3: bfloat16 [16, 64, 8, 128], P('dp', None, 'tp')
All inputs are finite; a program needn't handle non-finite values.
Results may differ from a plain program's by a relative error of at most 0.00825885.
Values sent between devices are 32-bit elements.
A program may use at most 768 MiB of HBM per device.

v0:
```python
import jax
import jax.numpy as jnp
from jax import lax
from jax.sharding import PartitionSpec as P

HEAD_DIM = 128
MASKED = -1e30


def rms_scale(tensor, norm_gain):
    mean_sq = jnp.mean(jnp.square(tensor), axis=-1, keepdims=True)
    return tensor * lax.rsqrt(mean_sq + 1e-6) * norm_gain


def rope_apply(tensor, positions):
    half_dim = HEAD_DIM // 2
    inv_freq = 1.0 / (1000000.0 ** (jnp.arange(half_dim, dtype=jnp.float32) * 2.0 / HEAD_DIM))
    angles = positions.astype(jnp.float32)[..., None] * inv_freq
    cos_t = jnp.cos(angles)[..., None, :]
    sin_t = jnp.sin(angles)[..., None, :]
    lead_half = tensor[..., :half_dim]
    tail_half = tensor[..., half_dim:]
    return jnp.concatenate([lead_half * cos_t - tail_half * sin_t, tail_half * cos_t + lead_half * sin_t], axis=-1)


def project_new(hidden, attn_norm, w_q, w_k, w_v, q_norm, k_norm, prefix_len):
    n_seq, n_new, d_model = hidden.shape
    kv_count = w_k.shape[1] // HEAD_DIM
    head_count = w_q.shape[1] // HEAD_DIM
    normed = rms_scale(hidden.astype(jnp.float32), attn_norm.astype(jnp.float32)).astype(jnp.bfloat16)
    q_lin = jnp.einsum('bce,ef->bcf', normed, w_q, preferred_element_type=jnp.float32).astype(jnp.bfloat16)
    k_lin = jnp.einsum('bce,ef->bcf', normed, w_k, preferred_element_type=jnp.float32).astype(jnp.bfloat16)
    v_lin = jnp.einsum('bce,ef->bcf', normed, w_v, preferred_element_type=jnp.float32).astype(jnp.bfloat16)
    positions = prefix_len[:, None] + jnp.arange(n_new, dtype=jnp.int32)[None, :]
    q_heads = q_lin.reshape(n_seq, n_new, head_count, HEAD_DIM).astype(jnp.float32)
    k_heads = k_lin.reshape(n_seq, n_new, kv_count, HEAD_DIM).astype(jnp.float32)
    q_rot = rope_apply(rms_scale(q_heads, q_norm.astype(jnp.float32)), positions).astype(jnp.bfloat16)
    k_new = rope_apply(rms_scale(k_heads, k_norm.astype(jnp.float32)), positions).astype(jnp.bfloat16)
    v_new = v_lin.reshape(n_seq, n_new, kv_count, HEAD_DIM)
    q_grp = q_rot.reshape(n_seq, n_new, kv_count, head_count // kv_count, HEAD_DIM)
    return q_grp, k_new, v_new


def attend_partial(q_grp, k_cache, v_cache, k_new, v_new, slot_ok, own_ok):
    score_scale = HEAD_DIM ** -0.5
    s_cache = jnp.einsum('bckgd,bpkd->bkcgp', q_grp, k_cache, preferred_element_type=jnp.float32) * score_scale
    s_cache = jnp.where(slot_ok[:, None, None, None, :], s_cache, MASKED)
    s_own = jnp.einsum('bckgd,bikd->bkcgi', q_grp, k_new, preferred_element_type=jnp.float32) * score_scale
    s_own = jnp.where(own_ok[None, None, :, None, :], s_own, MASKED)
    row_max = jnp.maximum(jnp.max(s_cache, axis=-1), jnp.max(s_own, axis=-1))
    p_cache = jnp.exp(s_cache - row_max[..., None])
    p_own = jnp.exp(s_own - row_max[..., None])
    row_sum = jnp.sum(p_cache, axis=-1) + jnp.sum(p_own, axis=-1)
    weighted = jnp.einsum('bkcgp,bpkd->bkcgd', p_cache.astype(jnp.bfloat16), v_cache, preferred_element_type=jnp.float32)
    weighted = weighted + jnp.einsum('bkcgi,bikd->bkcgd', p_own.astype(jnp.bfloat16), v_new, preferred_element_type=jnp.float32)
    return row_max, row_sum, weighted


def out_partial(attn_out, w_o):
    kv_count = attn_out.shape[1]
    group_size = attn_out.shape[3]
    w_heads = w_o.reshape(kv_count, group_size, HEAD_DIM, w_o.shape[1])
    return jnp.einsum('bkcgd,kgde->bce', attn_out, w_heads, preferred_element_type=jnp.float32)


def solution(mesh):
    def per_device(hidden, prefix_len, k_cache, v_cache, attn_norm, w_q, w_k, w_v, w_o, q_norm, k_norm):
        n_new = hidden.shape[1]
        cache_slots = k_cache.shape[1]
        cp_index = lax.axis_index('cp')
        q_grp, k_new, v_new = project_new(hidden, attn_norm, w_q, w_k, w_v, q_norm, k_norm, prefix_len)
        slot_ids = cp_index * cache_slots + jnp.arange(cache_slots)
        slot_ok = slot_ids[None, :] < prefix_len[:, None]
        new_ids = jnp.arange(n_new)
        own_ok = (new_ids[:, None] >= new_ids[None, :]) & (cp_index == 0)
        row_max, row_sum, weighted = attend_partial(q_grp, k_cache, v_cache, k_new, v_new, slot_ok, own_ok)
        glob_max = lax.pmax(row_max, 'cp')
        factor = jnp.exp(row_max - glob_max)
        total_w, total_sum = lax.psum((weighted * factor[..., None], row_sum * factor), 'cp')
        attn_out = (total_w / total_sum[..., None]).astype(jnp.bfloat16)
        out_proj = lax.psum(out_partial(attn_out, w_o), 'tp')
        block_out = (hidden.astype(jnp.float32) + out_proj).astype(jnp.bfloat16)
        return block_out, k_new, v_new

    cache_spec = P('dp', 'cp', 'tp', None)
    arg_specs = (P('dp', None, None), P('dp'), cache_spec, cache_spec, P(None), P(None, 'tp'), P(None, 'tp'), P(None, 'tp'), P('tp', None), P(None), P(None))
    out_specs = (P('dp', None, None), P('dp', None, 'tp', None), P('dp', None, 'tp', None))
    return jax.shard_map(per_device, mesh=mesh, in_specs=arg_specs, out_specs=out_specs, check_vma=False)
```

profile of v0, /device:TPU:97, one launch (start us, length us, event | category | flops | bytes accessed | tf_op | source)
XLA Modules:
  0.0 475.1 jit_solution(3619735276864044120)
XLA Ops:
  7.3 4.2 fusion.8
  11.6 0.7 copy-done.2
  12.3 1.9 fusion.43
  14.2 0.5 reshape.129
  14.8 1.2 multiply_reduce_fusion.1
  16.3 9.9 %fusion.29 = f32[16,64,768]{2,1,0:T(8,128)} fusion(bf16[3072,768]{1,0:T(8,128)(2,1)} %param.16, bf16[16,64,3072]{2,1,0:T(8,128)(2,1)} %param.11, f32[3072]{0:T(1024)S(1)} %convert_element_type.61, f32[16,64]{1,0:T(8,128)S(1)} %add_rsqrt_fusion.2), kind=kOutput, calls=%fused_computation.36 | convolution fusion | flops 4845993984 | bytes 14172160 | tf_op jit(solution)/shard_map/bce,ef->bcf/dot_general | solution.py:31
  26.2 4.6 reshape.128
  30.8 3.4 multiply_reduce_fusion
  34.7 0.3 fusion.53
  35.0 1.9 multiply_cosine_fusion
  36.9 3.6 multiply_multiply_fusion
  40.5 1.5 subtract_convert_fusion.1
  42.0 1.8 subtract_convert_fusion
  43.8 0.4 copy.62
  44.3 0.5 copy.63
  44.9 1.5 pad_maximum_fusion.1
  46.4 0.8 copy-done.3
  47.2 3.2 fusion.21
  50.4 24.8 %fusion = (f32[16,2,64,3]{2,3,1,0:T(4,128)S(1)}, f32[16,2,64,3,2048]{4,2,3,1,0:T(8,128)}) fusion(pred[16,2048]{1,0:T(8,128)(4,1)S(1)} %broadcast_compare_fusion, bf16[16,2048,2,128,1]{3,2,1,0,4:T(2,128)(2,1)} %bitcast.50, bf16[16,64,2,3,64]{4,1,3,2,0:T(8,128)(2,1)S(1)} %bitcast.54, bf16[16,64,2,3,64]{4,1,3,2,0:T(8,128)(2,1)S(1)} %bitcast.52), kind=kOutput, calls=%fused_computation.2 | convolution fusion | flops 3262113792 | bytes 68739072 | tf_op jit(solution)/shard_map/bckgd,bpkd->bkcgp/dot_general | solution.py:46
  75.3 24.5 %pmax.7 = f32[16,2,64,3]{2,3,1,0:T(4,128)S(1)} all-reduce(f32[16,2,64,3]{2,3,1,0:T(4,128)S(1)} %max.9), channel_id=1, replica_groups=mesh['dp'=1,'tp'=4,'cp'=8] {'cp'}, use_global_device_ids=true, to_apply=%region_5.6 | all-reduce | flops 6144 | bytes 49152 | tf_op jit(solution)/shard_map/pmax | solution.py:77
  99.8 3.0 fusion.22
  102.8 25.8 %fusion.1 = (f32[16,2,64,3]{2,3,1,0:T(4,128)S(1)}, bf16[16,2,64,3,2048]{4,2,3,1,0:T(8,128)(2,1)}) fusion(f32[16,2,64,3,2048]{4,2,3,1,0:T(8,128)} %get-tuple-element.31, f32[16,2,64,3]{2,3,1,0:T(4,128)S(1)} %max.9, pred[16,2048]{1,0:T(8,128)(4,1)S(1)} %broadcast_compare_fusion), kind=kLoop, calls=%fused_computation.3 | loop fusion | flops 62908416 | bytes 75579392 | tf_op jit(solution)/shard_map/reduce_sum | solution.py:53
  128.7 4.7 fusion.48
  133.5 18.6 %fusion.3 = f32[16,2,64,3,128]{4,2,1,3,0:T(8,128)} fusion(bf16[16,2,64,3,2048]{4,2,3,1,0:T(8,128)(2,1)} %get-tuple-element.21, bf16[16,2048,2,128,1]{3,2,1,0,4:T(2,128)(2,1)} %bitcast.56), kind=kOutput, calls=%fused_computation.5 | convolution fusion | flops 3221225472 | bytes 45088768 | tf_op jit(solution)/shard_map/bkcgp,bpkd->bkcgd/dot_general | solution.py:54
  152.1 4.0 add_multiply_fusion
  156.3 25.2 %psum.22 = f32[16,2,64,3]{2,3,1,0:T(4,128)S(1)} all-reduce(f32[16,2,64,3]{2,3,1,0:T(4,128)S(1)} %get-tuple-element.18), channel_id=1, replica_groups=mesh['dp'=1,'tp'=4,'cp'=8] {'cp'}, use_global_device_ids=true, to_apply=%region_9.10 | all-reduce | flops 6144 | bytes 49152 | tf_op jit(solution)/shard_map/psum | solution.py:79
  181.5 40.3 %all-reduce.3.cloned.1.call-done = f32[16,2,64,3,128]{4,2,1,3,0:T(8,128)} async-done(((f32[16,2,64,3,128]{4,2,1,3,0:T(8,128)}), f32[16,2,64,3,128]{4,2,1,3,0:T(8,128)}) %all-reduce.3.cloned.1.call-update) | async-done | bytes 3145744 | tf_op jit(solution)/shard_map/psum | solution.py:79
  221.8 10.6 %convolution_bitcast_fusion = f32[16,64,3072]{2,1,0:T(8,128)} fusion(bf16[2,3,128,3072,1]{3,2,1,0,4:T(8,128)(2,1)} %bitcast.57, f32[16,2,64,3,128]{4,2,1,3,0:T(8,128)} %all-reduce.3.cloned.1.call-done, f32[16,2,64,3]{2,1,3,0:T(2,128)S(1)} %copy.73), kind=kOutput, calls=%fused_computation.17 | convolution fusion | flops 4833411072 | bytes 20471808 | tf_op jit(solution)/shard_map/bkcgd,kgde->bce/dot_general | solution.py:63
  232.5 1.0 copy-done.4
  233.5 1.3 copy.76
  234.8 221.9 %all-reduce.5.cloned.1.call-done = f32[16,64,3072]{2,1,0:T(8,128)} async-done(((f32[16,64,3072]{2,1,0:T(8,128)}), f32[16,64,3072]{2,1,0:T(8,128)}) %all-reduce.5.cloned.1.call-update) | async-done | bytes 12582928 | tf_op jit(solution)/shard_map/psum | solution.py:81
  456.7 11.5 %fusion.11 = bf16[16,64,3072]{2,1,0:T(8,128)(2,1)} fusion(f32[16,64,3072]{2,1,0:T(8,128)} %all-reduce.5.cloned.1.call-done, bf16[16,64,3072]{2,1,0:T(8,128)(2,1)} %param.11), kind=kLoop, calls=%fused_computation.16 | loop fusion | flops 9437184 | bytes 25165824 | tf_op jit(solution)/shard_map/convert_element_type | solution.py:82
  (43 shorter events, 1.5 us)
Async XLA Ops:
  7.2 4.4 copy-start
  7.2 4.4 copy-start.6
  7.2 214.6 %all-reduce.3.cloned.1.call-start = ((), (), s32[]{:S(2)}) async-start(), calls=%async_computation | async-start | bytes 6291456 | tf_op jit(solution)/shard_map/psum | solution.py:79
  7.3 5.0 %copy-start.2 = (bf16[16,64,3072]{2,1,0:T(8,128)(2,1)S(1)}, bf16[16,64,3072]{2,1,0:T(8,128)(2,1)}, u32[]{:S(2)}) copy-start(bf16[16,64,3072]{2,1,0:T(8,128)(2,1)} %param.11) | copy-start | bytes 18874372
  14.2 2.0 copy-start.9
  14.2 2.0 copy-start.7
  30.8 3.9 copy-start.10
  46.4 0.8 copy-start.3
  102.8 25.9 %copy-start.8 = (bf16[3072,256]{1,0:T(8,128)(2,1)S(1)}, bf16[3072,256]{1,0:T(8,128)(2,1)}, u32[]{:S(2)}) copy-start(bf16[3072,256]{1,0:T(8,128)(2,1)} %param.18) | copy-start | bytes 4718596
  133.5 18.6 %copy-start.5 = (bf16[16,64,2,128]{3,2,1,0:T(2,128)(2,1)}, bf16[16,64,2,128]{3,2,1,0:T(2,128)(2,1)S(1)}, u32[]{:S(2)}) copy-start(bf16[16,64,2,128]{3,2,1,0:T(2,128)(2,1)S(1)} %reshape.126) | copy-start | bytes 1572868
  156.2 300.5 %all-reduce.5.cloned.1.call-start = ((), (), s32[]{:S(2)}) async-start(), calls=%async_computation.1 | async-start | bytes 25165824 | tf_op jit(solution)/shard_map/psum | solution.py:81
  232.4 1.0 copy-start.4
  456.7 11.5 %copy-start.1 = (bf16[3072,256]{1,0:T(8,128)(2,1)S(1)}, bf16[3072,256]{1,0:T(8,128)(2,1)}, u32[]{:S(2)}) copy-start(bf16[3072,256]{1,0:T(8,128)(2,1)} %param.17) | copy-start | bytes 4718596
Sparse Core Ops, SparseCore 0:
  156.4 65.3 all-reduce.2
  232.6 224.0 all-reduce.4
where the time goes:
time: 476 us; the launch traced here: 475 us
  waiting for transfers between devices  262 us (55%)
  matrix products  77.8 us (16%)
  other arithmetic  60 us (13%)
  blocking collectives  49.7 us (10%)
  between operations  14.4 us (3%)
  local copies, waits for them, and re-layouts  10.7 us (2%)
    psum x1, waiting for transfers between devices, per_device(): out_proj = lax.psum(out_partial(attn_out, w_o), 'tp')  222 us
    psum x1, waiting for transfers between devices, per_device(): lax.psum((weighted * factor[..., None], row_sum * factor), 'cp')  40.3 us
    reduce_sum x2, other arithmetic, attend_partial(): row_sum = jnp.sum(p_cache, axis=-1) + jnp.sum(p_own, axis=-1)  28.8 us
    psum x1, blocking collectives, per_device(): lax.psum((weighted * factor[..., None], row_sum * factor), 'cp')  25.2 us
    dot_general x1, matrix products, attend_partial(): jnp.einsum('bckgd,bpkd->bkcgp', q_grp, k_cache, preferred_element_type=jn...  24.8 us
    pmax x1, blocking collectives, per_device(): glob_max = lax.pmax(row_max, 'cp')  24.5 us
    dot_general x1, matrix products, attend_partial(): jnp.einsum('bkcgp,bpkd->bkcgd', p_cache.astype(jnp.bfloat16), v_cache, pr...  18.6 us
    convert_element_type x1, other arithmetic, per_device(): block_out = (hidden.astype(jnp.float32) + out_proj).astype(jnp.bfloat16)  11.5 us
  transfers between devices with their start and end apart: 2, of which 2 were waited for; matrix products, arithmetic and copies ran while one was open for 0% of the time, Pallas kernels for 0%

commit v1 on v0

v1 whole, which is shorter than its diff:
```python
import functools

import jax
import jax.numpy as jnp
from jax import lax
from jax.experimental import pallas as pl
from jax.experimental.pallas import tpu as pltpu
from jax.sharding import PartitionSpec as P

HEAD_DIM = 128
MASKED = -1e30
LOW = -3e38
EXP_SCALE = (HEAD_DIM ** -0.5) * 1.4426950408889634
WAVES = 2
STAT_ROWS = 8
MESH = pl.DeviceIdType.MESH
F32 = jnp.float32
BF16 = jnp.bfloat16


def rms_scale(tensor, norm_gain):
    mean_sq = jnp.mean(jnp.square(tensor), axis=-1, keepdims=True)
    return tensor * lax.rsqrt(mean_sq + 1e-6) * norm_gain


def rope_apply(tensor, positions):
    half_dim = HEAD_DIM // 2
    inv_freq = 1.0 / (1000000.0 ** (jnp.arange(half_dim, dtype=F32) * 2.0 / HEAD_DIM))
    angles = positions.astype(F32)[..., None] * inv_freq
    cos_t = jnp.cos(angles)[..., None, :]
    sin_t = jnp.sin(angles)[..., None, :]
    lead_half = tensor[..., :half_dim]
    tail_half = tensor[..., half_dim:]
    return jnp.concatenate([lead_half * cos_t - tail_half * sin_t, tail_half * cos_t + lead_half * sin_t], axis=-1)


def project_new(hidden, attn_norm, w_q, w_k, w_v, q_norm, k_norm, prefix_len):
    n_seq, n_new, d_model = hidden.shape
    kv_count = w_k.shape[1] // HEAD_DIM
    head_count = w_q.shape[1] // HEAD_DIM
    normed = rms_scale(hidden.astype(F32), attn_norm.astype(F32)).astype(BF16)
    q_lin = jnp.einsum('bce,ef->bcf', normed, w_q, preferred_element_type=F32).astype(BF16)
    k_lin = jnp.einsum('bce,ef->bcf', normed, w_k, preferred_element_type=F32).astype(BF16)
    v_lin = jnp.einsum('bce,ef->bcf', normed, w_v, preferred_element_type=F32).astype(BF16)
    positions = prefix_len[:, None] + jnp.arange(n_new, dtype=jnp.int32)[None, :]
    q_heads = q_lin.reshape(n_seq, n_new, head_count, HEAD_DIM).astype(F32)
    k_heads = k_lin.reshape(n_seq, n_new, kv_count, HEAD_DIM).astype(F32)
    q_rot = rope_apply(rms_scale(q_heads, q_norm.astype(F32)), positions).astype(BF16)
    k_new = rope_apply(rms_scale(k_heads, k_norm.astype(F32)), positions).astype(BF16)
    return q_rot.reshape(n_seq, n_new, head_count * HEAD_DIM), k_new.reshape(n_seq, n_new, kv_count * HEAD_DIM), v_lin


def block_diag(pair):
    zero = jnp.zeros((pair.shape[0], HEAD_DIM), pair.dtype)
    top = jnp.concatenate([pair[:, :HEAD_DIM], zero], axis=1)
    low = jnp.concatenate([zero, pair[:, HEAD_DIM:]], axis=1)
    return jnp.concatenate([top, low], axis=0)


def dot_nt(a, b):
    return lax.dot_general(a, b, (((1,), (1,)), ((), ())), preferred_element_type=F32)


def attend_seq(q_tok, k_ref, v_ref, k_own, v_own, limit, own_on, score_ref, even_ref, odd_ref, write_out):
    n_new = q_tok.shape[0]
    group = q_tok.shape[1] // (2 * HEAD_DIM)
    rows = group * n_new
    n_keys = k_ref.shape[0]
    chunk = even_ref.shape[0]
    q_ext = jnp.concatenate([
        jnp.concatenate([q_tok[:, g * HEAD_DIM:(g + 1) * HEAD_DIM], q_tok[:, (group + g) * HEAD_DIM:(group + g + 1) * HEAD_DIM]], axis=1)
        for g in range(group)], axis=0)
    lane = lax.broadcasted_iota(jnp.int32, (rows, HEAD_DIM), 1)
    is_even = lane % 2 == 0
    key_lane = lax.broadcasted_iota(jnp.int32, (1, chunk), 1)
    run_max = jnp.full((rows, HEAD_DIM), MASKED, F32)
    for start in range(0, n_keys, chunk):
        keys = k_ref[pl.ds(start, chunk), :]
        keys_ext = jnp.concatenate([keys * even_ref[...], keys * odd_ref[...]], axis=1)
        scores = dot_nt(q_ext, keys_ext)
        scores = jnp.where(key_lane < 2 * limit - start, scores, MASKED)
        score_ref[:, pl.ds(start, chunk)] = scores
        for block in range(0, chunk, HEAD_DIM):
            run_max = jnp.maximum(run_max, scores[:, block:block + HEAD_DIM])
    s_own = dot_nt(q_ext, block_diag(k_own))
    own_row = lax.broadcasted_iota(jnp.int32, (rows, 2 * n_new), 0) % n_new
    own_lane = lax.broadcasted_iota(jnp.int32, (rows, 2 * n_new), 1)
    own_first = own_lane < n_new
    own_key = jnp.where(own_first, own_lane, own_lane - n_new)
    s_own = jnp.where((own_key <= own_row) & own_on, s_own, MASKED)
    max_0 = jnp.maximum(jnp.max(jnp.where(is_even, run_max, LOW), axis=1, keepdims=True),
                        jnp.max(jnp.where(own_first, s_own, LOW), axis=1, keepdims=True))
    max_1 = jnp.maximum(jnp.max(jnp.where(is_even, LOW, run_max), axis=1, keepdims=True),
                        jnp.max(jnp.where(own_first, LOW, s_own), axis=1, keepdims=True))
    max_lane = jnp.where(is_even, max_0, max_1)
    p_own = jnp.exp2((s_own - jnp.where(own_first, max_0, max_1)) * EXP_SCALE)
    acc = jnp.dot(p_own.astype(BF16), block_diag(v_own), preferred_element_type=F32)
    run_sum = jnp.zeros((rows, HEAD_DIM), F32)
    for start in range(0, n_keys, chunk):
        probs = []
        for block in range(start, start + chunk, HEAD_DIM):
            p_blk = jnp.exp2((score_ref[:, pl.ds(block, HEAD_DIM)] - max_lane) * EXP_SCALE)
            run_sum = run_sum + p_blk
            probs.append(p_blk.astype(BF16))
        vals = v_ref[pl.ds(start, chunk), :]
        vals_ext = jnp.concatenate([vals * even_ref[...], vals * odd_ref[...]], axis=1)
        acc = acc + jnp.dot(jnp.concatenate(probs, axis=1), vals_ext, preferred_element_type=F32)
    sum_0 = jnp.sum(jnp.where(is_even, run_sum, 0.0) + jnp.where(own_first, p_own, 0.0), axis=1, keepdims=True)
    sum_1 = jnp.sum(jnp.where(is_even, 0.0, run_sum) + jnp.where(own_first, 0.0, p_own), axis=1, keepdims=True)
    stat = jnp.where(lane == 0, max_0, jnp.where(lane == 1, max_1, jnp.where(lane == 2, sum_0, sum_1)))
    stat = jnp.concatenate([stat, jnp.zeros((2 * HEAD_DIM - rows, HEAD_DIM), F32)], axis=0)
    write_out(acc, stat.T[:STAT_ROWS])


def attend_kernel(len_ref, q_ref, kn_ref, vn_ref, k_hbm, v_hbm, out_ref, k_buf, v_buf, score_ref, even_ref, odd_ref, k_sem, v_sem):
    n_seq, n_keys = k_hbm.shape[0], k_hbm.shape[1]
    per_wave = n_seq // WAVES
    cp_index = lax.axis_index('cp')
    row = lax.broadcasted_iota(jnp.int32, even_ref.shape, 0)
    odd = (row % 2).astype(F32)
    odd_ref[...] = odd.astype(BF16)
    even_ref[...] = (1.0 - odd).astype(BF16)

    def seq_of(i):
        return (i // per_wave) * per_wave + 2 * (i % (per_wave // 2)) + (i % per_wave) // (per_wave // 2)

    def copies(i, slot):
        b = seq_of(i)
        return (pltpu.make_async_copy(k_hbm.at[b], k_buf.at[slot], k_sem.at[slot]),
                pltpu.make_async_copy(v_hbm.at[b], v_buf.at[slot], v_sem.at[slot]))

    for cp in copies(0, 0):
        cp.start()

    def step(i, carry):
        slot = i % 2
        b = seq_of(i)

        @pl.when(i + 1 < n_seq)
        def _():
            for cp in copies(i + 1, 1 - slot):
                cp.start()
        for cp in copies(i, slot):
            cp.wait()
        limit = len_ref[b] - cp_index * (n_keys // 2)

        def write_out(acc, stat):
            rows = acc.shape[0]
            out_ref[i, pl.ds(0, rows), :] = acc
            out_ref[i, pl.ds(rows, STAT_ROWS), :] = stat
        attend_seq(q_ref[b], k_buf.at[slot], v_buf.at[slot], kn_ref[b], vn_ref[b], limit, cp_index == 0, score_ref, even_ref, odd_ref, write_out)
        return carry
    lax.fori_loop(0, n_seq, step, 0)


def attend(prefix_len, q_tok, k_new, v_new, k_cache, v_cache):
    n_seq, n_new, q_width = q_tok.shape
    n_keys = k_cache.shape[1]
    rows = n_new * q_width // (2 * HEAD_DIM)
    chunk = min(512, n_keys)
    vmem = pl.BlockSpec(memory_space=pltpu.VMEM)
    hbm = pl.BlockSpec(memory_space=pl.ANY)
    return pl.pallas_call(
        attend_kernel,
        out_shape=jax.ShapeDtypeStruct((n_seq, rows + STAT_ROWS, 2 * HEAD_DIM), F32),
        in_specs=[pl.BlockSpec(memory_space=pltpu.SMEM), vmem, vmem, vmem, hbm, hbm],
        out_specs=vmem,
        scratch_shapes=[pltpu.VMEM((2, n_keys, HEAD_DIM), BF16), pltpu.VMEM((2, n_keys, HEAD_DIM), BF16),
                        pltpu.VMEM((rows, n_keys), F32), pltpu.VMEM((chunk, HEAD_DIM), BF16), pltpu.VMEM((chunk, HEAD_DIM), BF16),
                        pltpu.SemaphoreType.DMA((2,)), pltpu.SemaphoreType.DMA((2,))],
        compiler_params=pltpu.CompilerParams(vmem_limit_bytes=48 * 1024 * 1024),
        name='attend',
    )(prefix_len, q_tok, k_new, v_new, k_cache, v_cache)


def merge_units(units, rows, normalise):
    stats = [u[rows:rows + STAT_ROWS] for u in units]
    peak = functools.reduce(jnp.maximum, [s[0:2] for s in stats])
    facs = [jnp.exp2((s[0:2] - peak) * EXP_SCALE) for s in stats]
    total = functools.reduce(jnp.add, [s[2:4] * f for s, f in zip(stats, facs)])
    if normalise:
        facs = [f / total for f in facs]
    table = jnp.concatenate(facs, axis=0)
    table = jnp.concatenate([table, jnp.zeros((HEAD_DIM - table.shape[0], table.shape[1]), F32)], axis=0).T
    heads = []
    for h in range(2):
        parts = [u[:rows, h * HEAD_DIM:(h + 1) * HEAD_DIM] * table[:rows, 2 * i + h:2 * i + h + 1] for i, u in enumerate(units)]
        heads.append(functools.reduce(jnp.add, parts))
    stat = jnp.concatenate([peak, total, jnp.zeros((STAT_ROWS - 4, total.shape[1]), F32)], axis=0)
    return jnp.concatenate(heads, axis=1), stat


class Exchange:
    def __init__(self, wave, refs, n_cp, n_tp):
        self.w = wave
        self.r = refs
        self.n_x = n_cp // 2
        self.n_cp = n_cp
        self.n_tp = n_tp
        self.cp = lax.axis_index('cp')
        self.tp = lax.axis_index('tp')
        self.x = self.cp // 2
        self.core = self.cp % 2
        self.pending = []

    def cp_at(self, dx):
        return lax.rem(self.cp + 2 * dx + self.n_cp, self.n_cp)

    def tp_at(self, dy):
        return lax.rem(self.tp + dy + self.n_tp, self.n_tp)

    def send(self, src, dst, recv_sem, cp=None, tp=None):
        self.r['count'][0] += 1
        where = {}
        if cp is not None:
            where['cp'] = cp
        if tp is not None:
            where['tp'] = tp
        copy = pltpu.make_async_remote_copy(src_ref=src, dst_ref=dst, send_sem=self.r['send'].at[self.r['count'][0] - 1], recv_sem=recv_sem,
                                            device_id=where, device_id_type=MESH)
        copy.start()
        self.pending.append(copy)

    def wait(self, dst, recv_sem):
        pltpu.make_async_remote_copy(src_ref=dst, dst_ref=dst, send_sem=self.r['send'].at[0], recv_sem=recv_sem,
                                     device_id={'cp': self.cp}, device_id_type=MESH).wait_recv()

    @property
    def partner(self):
        return self.cp + 1 - 2 * self.core

    def pair_send(self):
        r, w = self.r, self.w
        self.send(r['sums'].at[w, 1 - self.core], r['pair'].at[w], r['pair_sem'].at[w], cp=self.partner)

    def pair_merge(self):
        r, w, rows = self.r, self.w, self.r['rows']
        self.wait(r['pair'].at[w], r['pair_sem'].at[w])
        for d in (2, 1, 3, 0):
            ox = lax.rem(self.x + d, self.n_x)
            merged, stat = merge_units([r['pair'][w, ox], r['sums'][w, self.core, ox]], rows, False)
            r['pair'][w, ox, pl.ds(0, rows), :] = merged
            r['pair'][w, ox, pl.ds(rows, STAT_ROWS), :] = stat
            if d:
                self.send(r['pair'].at[w, ox], r['xin'].at[w, d - 1], r['xin_sem'].at[w, d - 1], cp=self.cp_at(d))

    def project_out(self):
        r, w, rows = self.r, self.w, self.r['rows']
        for d in range(1, self.n_x):
            self.wait(r['xin'].at[w, d - 1], r['xin_sem'].at[w, d - 1])
        units = [r['pair'][w, self.x]] + [r['xin'][w, d - 1] for d in range(1, self.n_x)]
        attn, _ = merge_units(units, rows, True)
        attn = attn.astype(BF16)
        n_new = r['n_new']
        group = rows // n_new
        lhs = jnp.concatenate([attn[g * n_new:(g + 1) * n_new, k * HEAD_DIM:(k + 1) * HEAD_DIM] for k in range(2) for g in range(group)], axis=1)
        width = r['wo'].shape[1] // self.n_tp
        for d in (2, 1, 3, 0):
            oy = lax.rem(self.tp + d, self.n_tp)
            for part in range(0, width, 256):
                cols = pl.ds(pl.multiple_of(oy * width + part, 128), 256)
                r['yout'][w, oy, :, pl.ds(part, 256)] = jnp.dot(lhs, r['wo'][:, cols], preferred_element_type=F32)
            if d:
                self.send(r['yout'].at[w, oy], r['yin'].at[w, d - 1], r['yin_sem'].at[w, d - 1], tp=self.tp_at(d))

    def finish_rows(self):
        r, w = self.r, self.w
        for d in range(1, self.n_tp):
            self.wait(r['yin'].at[w, d - 1], r['yin_sem'].at[w, d - 1])
        width = r['wo'].shape[1] // self.n_tp
        seq = w * self.n_cp + self.cp
        total = r['yout'][w, self.tp]
        for d in range(1, self.n_tp):
            total = total + r['yin'][w, d - 1]
        cols = pl.ds(pl.multiple_of(self.tp * width, 128), width)
        total = total + r['x'][seq, :, cols].astype(F32)
        r['gather'][w, self.cp, self.tp] = total.astype(BF16).astype(F32)

    def unit(self, half, rx, ry, sub=None):
        n_half = self.r['n_new'] // 2
        start, size = half * n_half, n_half
        if sub is not None:
            start, size = start + sub * (n_half // 2), n_half // 2
        return self.r['gather'].at[self.w, self.cp_at(rx), self.tp_at(ry), pl.ds(start, size), :]

    def hop(self, half, rx, ry, axis, step, sub=None):
        ref = self.unit(half, rx, ry, sub)
        tx, ty = (rx - step) % self.n_x, ry
        if axis == 'y':
            tx, ty = rx, (ry - step) % self.n_tp
        sem = self.r['gather_sem'].at[self.w, half, tx, ty, sub or 0]
        if axis == 'x':
            self.send(ref, ref, sem, cp=self.cp_at(step))
        else:
            self.send(ref, ref, sem, tp=self.tp_at(step))

    def arrive(self, half, rx, ry, sub=None):
        self.wait(self.unit(half, rx, ry, sub), self.r['gather_sem'].at[self.w, half, rx, ry, sub or 0])

    def share(self, half, rx, ry):
        ref = self.unit(half, rx, ry)
        self.send(ref, ref, self.r['share_sem'].at[self.w, half, rx, ry], cp=self.partner)

    def first(self, half):
        return ('x', 'y') if half == 0 else ('y', 'x')

    def at(self, half, a, b):
        return (a, b) if half == 0 else (b, a)

    def gather_start(self):
        for half in (0, 1):
            one, two = self.first(half)
            for axis in (one, two):
                for step in (1, -1):
                    self.hop(half, 0, 0, axis, step)
        for half in (0, 1):
            self.share(half, 0, 0)

    def gather_first(self):
        for a, step in ((3, 1), (1, -1)):
            for half in (0, 1):
                one, two = self.first(half)
                rx, ry = self.at(half, a, 0)
                self.arrive(half, rx, ry)
                self.hop(half, rx, ry, one, step, sub=0 if step == 1 else 1)
                self.hop(half, rx, ry, two, 1)
                self.hop(half, rx, ry, two, -1)
                self.share(half, rx, ry)

    def gather_opposite(self):
        for half in (0, 1):
            one, two = self.first(half)
            rx, ry = self.at(half, 2, 0)
            self.arrive(half, rx, ry, 0)
            self.arrive(half, rx, ry, 1)
            self.hop(half, rx, ry, two, 1)
            self.hop(half, rx, ry, two, -1)
            self.share(half, rx, ry)

    def gather_second(self):
        for a in (0, 3, 1, 2):
            for b, step in ((3, 1), (1, -1)):
                for half in (0, 1):
                    one, two = self.first(half)
                    rx, ry = self.at(half, a, b)
                    self.arrive(half, rx, ry)
                    self.hop(half, rx, ry, two, step, sub=0 if step == 1 else 1)
                    self.share(half, rx, ry)

    def gather_last(self):
        for a in (0, 3, 1, 2):
            for half in (0, 1):
                rx, ry = self.at(half, a, 2)
                self.arrive(half, rx, ry, 0)
                self.arrive(half, rx, ry, 1)
                self.share(half, rx, ry)

    def gather_shared(self):
        for half in (0, 1):
            for rx in range(self.n_x):
                for ry in range(self.n_tp):
                    n_half = self.r['n_new'] // 2
                    cp = self.cp_at(rx) + 1 - 2 * self.core
                    ref = self.r['gather'].at[self.w, cp, self.tp_at(ry), pl.ds(half * n_half, n_half), :]
                    self.wait(ref, self.r['share_sem'].at[self.w, half, rx, ry])

    def write_rows(self):
        r, w = self.r, self.w
        width = r['wo'].shape[1] // self.n_tp

        def body(s, carry):
            for ty in range(self.n_tp):
                r['stage'][s, :, pl.ds(ty * width, width)] = r['gather'][w, s, ty].astype(BF16)
            pltpu.make_async_copy(r['stage'].at[s], r['out'].at[w * self.n_cp + s], r['out_sem'].at[w]).start()
            return carry
        if w:
            pltpu.make_async_copy(r['stage'], r['out'].at[pl.ds((w - 1) * self.n_cp, self.n_cp)], r['out_sem'].at[w - 1]).wait()
        lax.fori_loop(0, self.n_cp, body, 0)
        if w == WAVES - 1:
            pltpu.make_async_copy(r['stage'], r['out'].at[pl.ds(w * self.n_cp, self.n_cp)], r['out_sem'].at[w]).wait()


def entry_barrier(n_cp, n_tp):
    cp, tp = lax.axis_index('cp'), lax.axis_index('tp')
    barrier = pltpu.get_barrier_semaphore()
    peers = [{'cp': cp + 1 - 2 * (cp % 2)}]
    peers += [{'cp': lax.rem(cp + 2 * d, n_cp)} for d in range(1, n_cp // 2)]
    peers += [{'tp': lax.rem(tp + d, n_tp)} for d in range(1, n_tp)]
    for peer in peers:
        pl.semaphore_signal(barrier, inc=1, device_id=peer, device_id_type=MESH)
    pl.semaphore_wait(barrier, len(peers))


def exchange_kernel(n_cp, n_tp, n_new, sums_ref, x_ref, wo_ref, out_ref, pair, xin, yout, yin, gather, stage,
                    send_sem, pair_sem, xin_sem, yin_sem, gather_sem, share_sem, out_sem):
    entry_barrier(n_cp, n_tp)
    refs = {'sums': sums_ref, 'x': x_ref, 'wo': wo_ref, 'out': out_ref, 'pair': pair, 'xin': xin, 'yout': yout, 'yin': yin,
            'gather': gather, 'stage': stage, 'send': send_sem, 'pair_sem': pair_sem, 'xin_sem': xin_sem, 'yin_sem': yin_sem,
            'gather_sem': gather_sem, 'share_sem': share_sem, 'out_sem': out_sem, 'n_new': n_new, 'rows': sums_ref.shape[3] - STAT_ROWS,
            'count': [0]}
    waves = [Exchange(w, refs, n_cp, n_tp) for w in range(WAVES)]
    for name in ('pair_send', 'pair_merge', 'project_out', 'finish_rows+gather_start', 'gather_first', 'gather_opposite', 'gather_second',
                 'gather_last', 'gather_shared+write_rows'):
        for wave in waves:
            for part in name.split('+'):
                getattr(wave, part)()
    for wave in waves:
        for copy in wave.pending:
            copy.wait_send()


def exchange(sums, hidden, w_o, n_cp, n_tp):
    n_seq, n_new, d_model = hidden.shape
    unit_rows, unit_lanes = sums.shape[1:]
    n_x = n_cp // 2
    width = d_model // n_tp
    vmem = pl.BlockSpec(memory_space=pltpu.VMEM)
    n_send = WAVES * (1 + (n_x - 1) + (n_tp - 1) + 40 + 32)
    return pl.pallas_call(
        functools.partial(exchange_kernel, n_cp, n_tp, n_new),
        out_shape=jax.ShapeDtypeStruct((n_seq, n_new, d_model), BF16),
        in_specs=[vmem, vmem, vmem],
        out_specs=pl.BlockSpec(memory_space=pl.ANY),
        scratch_shapes=[
            pltpu.VMEM((WAVES, n_x, unit_rows, unit_lanes), F32),
            pltpu.VMEM((WAVES, n_x - 1, unit_rows, unit_lanes), F32),
            pltpu.VMEM((WAVES, n_tp, n_new, width), F32),
            pltpu.VMEM((WAVES, n_tp - 1, n_new, width), F32),
            pltpu.VMEM((WAVES, n_cp, n_tp, n_new, width), F32),
            pltpu.VMEM((n_cp, n_new, d_model), BF16),
            pltpu.SemaphoreType.DMA((n_send,)),
            pltpu.SemaphoreType.DMA((WAVES,)),
            pltpu.SemaphoreType.DMA((WAVES, n_x - 1)),
            pltpu.SemaphoreType.DMA((WAVES, n_tp - 1)),
            pltpu.SemaphoreType.DMA((WAVES, 2, n_x, n_tp, 2)),
            pltpu.SemaphoreType.DMA((WAVES, 2, n_x, n_tp)),
            pltpu.SemaphoreType.DMA((WAVES,)),
        ],
        compiler_params=pltpu.CompilerParams(collective_id=0, has_side_effects=True, vmem_limit_bytes=60 * 1024 * 1024),
        name='exchange',
    )(sums.reshape(WAVES, 2, n_x, unit_rows, unit_lanes), hidden, w_o)


def solution(mesh):
    n_cp, n_tp = mesh.shape['cp'], mesh.shape['tp']

    def per_device(hidden, prefix_len, k_cache, v_cache, attn_norm, w_q, w_k, w_v, w_o, q_norm, k_norm):
        n_seq, n_new, _ = hidden.shape
        slots = k_cache.shape[1]
        q_tok, k_new, v_new = project_new(hidden, attn_norm, w_q, w_k, w_v, q_norm, k_norm, prefix_len)
        sums = attend(prefix_len, q_tok, k_new, v_new, k_cache.reshape(n_seq, slots * 2, HEAD_DIM), v_cache.reshape(n_seq, slots * 2, HEAD_DIM))
        block_out = exchange(sums, hidden, w_o, n_cp, n_tp)
        return block_out, k_new.reshape(n_seq, n_new, 2, HEAD_DIM), v_new.reshape(n_seq, n_new, 2, HEAD_DIM)

    cache_spec = P('dp', 'cp', 'tp', None)
    arg_specs = (P('dp', None, None), P('dp'), cache_spec, cache_spec, P(None), P(None, 'tp'), P(None, 'tp'), P(None, 'tp'), P('tp', None), P(None), P(None))
    out_specs = (P('dp', None, None), P('dp', None, 'tp', None), P('dp', None, 'tp', None))
    return jax.shard_map(per_device, mesh=mesh, in_specs=arg_specs, out_specs=out_specs, check_vma=False)
```

time: 476 us -> 198 us (0.42)
  waiting for transfers between devices: 262 us -> 0 us
  Pallas kernels: 0 us -> 133 us
  matrix products: 77.8 us -> 17.7 us
  blocking collectives: 49.7 us -> 0 us
  other arithmetic: 60 us -> 26.4 us
  between operations: 14.4 us -> 0.85 us
  local copies, waits for them, and re-layouts: 10.7 us -> 19.8 us
    psum x2 -> x0, waiting for transfers between devices: 262 us -> none  [the longest x1 222 us: per_device(): out_proj = lax.psum(out_partial(attn_out, w_o), 'tp')]
    pallas_call x0 -> x2, Pallas kernels: none -> 133 us  [the longest x1 84.9 us: exchange(): pl.pallas_call(functools.partial(exchange_kernel, n_cp, n_tp, n_new), out...]
    dot_general x8 -> x3, matrix products: 77.8 us -> 17.7 us  [the longest x1 9.82 us: project_new(): jnp.einsum('bce,ef->bcf', normed, w_q, preferred_element_type=F32)]
    reduce_sum x2 -> x0, other arithmetic: 28.8 us -> none  [attend_partial(): row_sum = jnp.sum(p_cache, axis=-1) + jnp.sum(p_own, axis=-1)]
    psum x1 -> x0, blocking collectives: 25.2 us -> none  [per_device(): lax.psum((weighted * factor[..., None], row_sum * factor), 'cp')]
    pmax x1 -> x0, blocking collectives: 24.5 us -> none  [per_device(): glob_max = lax.pmax(row_max, 'cp')]
    convert_element_type x5, other arithmetic: 11.6 us -> 4.3 us  [the longest x1 1.42 us: project_new(): rope_apply(rms_scale(k_heads, k_norm.astype(F32)), positions).astype(BF16)]
    convert_element_type x2 -> x4, local copies, waits for them, and re-layouts: 5.11 us -> 10.2 us  [the longest x1 4.57 us: project_new(): q_heads = q_lin.reshape(n_seq, n_new, head_count, HEAD_DIM).astype(F32)]
  transfers between devices with their start and end apart: 2 -> 0, of which waited for: 2 -> 0; matrix products, arithmetic and copies ran while one was open for 0% -> 0% of each run, Pallas kernels for 0% -> 0%
where the time goes in v1:
time: 198 us
  Pallas kernels  133 us (67%)
  other arithmetic  26.4 us (13%)
  local copies, waits for them, and re-layouts  19.8 us (10%)
  matrix products  17.7 us (9%)
    pallas_call x1, Pallas kernels, exchange(): pl.pallas_call(functools.partial(exchange_kernel, n_cp, n_tp, n_new), out...  84.9 us
    pallas_call x1, Pallas kernels, attend(): pl.pallas_call(attend_kernel, out_shape=jax.ShapeDtypeStruct((n_seq, rows...  48.3 us
    dot_general x1, matrix products, project_new(): jnp.einsum('bce,ef->bcf', normed, w_q, preferred_element_type=F32)  9.82 us
    reduce_sum x3, other arithmetic, rms_scale(): mean_sq = jnp.mean(jnp.square(tensor), axis=-1, keepdims=True)  8.6 us
    unnamed x15, local copies, waits for them, and re-layouts  7.84 us
    dot_general x1, matrix products, project_new(): jnp.einsum('bce,ef->bcf', normed, w_k, preferred_element_type=F32)  6.04 us
    mul x2, other arithmetic, rms_scale(): return tensor * lax.rsqrt(mean_sq + 1e-06) * norm_gain  5.16 us
    convert_element_type x1, local copies, waits for them, and re-layouts, project_new(): q_heads = q_lin.reshape(n_seq, n_new, head_count, HEAD_DIM).astype(F32)  4.57 us

profile of v1, /device:TPU:97, one launch (start us, length us, event | category | flops | bytes accessed | tf_op | source)
XLA Modules:
  0.0 198.0 jit_solution(5486459938212566437)
XLA Ops:
  0.6 0.0 copy-start
  0.6 0.0 copy-start.4
  0.7 0.8 convert_element_type.62
  1.5 1.1 convert_element_type.68
  2.6 1.0 add_convert_fusion.1
  3.6 4.1 %fusion = f32[16,64]{1,0:T(8,128)S(1)} fusion(bf16[16,64,3072]{2,1,0:T(8,128)(2,1)} %x_ref.1), kind=kLoop, calls=%fused_computation.2 | loop fusion | flops 9436160 | bytes 6295552 | tf_op jit(solution)/shard_map/reduce_sum | solution.py:22
  7.7 1.9 fusion.32.vn_ref
  9.6 0.9 reshape.91
  10.5 1.9 multiply_cosine_fusion
  12.4 6.0 %fusion.27 = f32[16,64,256]{2,1,0:T(8,128)} fusion(bf16[3072,256]{1,0:T(8,128)(2,1)} %param.17, bf16[16,64,3072]{2,1,0:T(8,128)(2,1)} %x_ref.1, f32[3072]{0:T(1024)S(1)} %convert_element_type.57, f32[16,64]{1,0:T(8,128)S(1)} %add_rsqrt_fusion.2), kind=kOutput, calls=%fused_computation.19 | convolution fusion | flops 1623719936 | bytes 8929280 | tf_op jit(solution)/shard_map/bce,ef->bcf/dot_general | solution.py:43
  18.4 1.7 reshape.93
  20.2 1.2 multiply_reduce_fusion.1
  21.3 0.2 copy.18
  21.6 0.2 copy.19
  21.8 1.6 multiply_multiply_fusion.1
  23.4 1.7 multiply_subtract_fusion
  25.1 1.4 maximum_convert_fusion
  26.6 0.0 copy-start.5
  26.6 0.3 convert_element_type.70.kn_ref
  26.9 9.8 %fusion.15 = f32[16,64,768]{2,1,0:T(8,128)} fusion(bf16[3072,768]{1,0:T(8,128)(2,1)} %param.16, bf16[16,64,3072]{2,1,0:T(8,128)(2,1)} %x_ref.1, f32[3072]{0:T(1024)S(1)} %convert_element_type.57, f32[16,64]{1,0:T(8,128)S(1)} %add_rsqrt_fusion.2), kind=kOutput, calls=%fused_computation.15 | convolution fusion | flops 4845993984 | bytes 14172160 | tf_op jit(solution)/shard_map/bce,ef->bcf/dot_general | solution.py:42
  36.7 4.6 %reshape.92 = f32[16,64,6,128]{3,2,1,0:T(8,128)} reshape(f32[16,64,768]{2,1,0:T(8,128)} %fusion.15) | data formatting | bytes 6291456 | tf_op jit(solution)/shard_map/convert_element_type | solution.py:46
  41.3 3.4 %multiply_reduce_fusion = f32[16,64,6]{2,1,0:T(8,128)S(1)} fusion(f32[16,64,6,128]{3,2,1,0:T(8,128)} %reshape.92), kind=kLoop, calls=%fused_computation.10 | loop fusion | flops 1566720 | bytes 3170304 | tf_op jit(solution)/shard_map/reduce_sum | solution.py:22
  44.7 0.2 copy.16
  44.9 0.2 copy.17
  45.2 3.6 %multiply_multiply_fusion = f32[16,64,6,128]{3,2,1,0:T(8,128)S(1)} fusion(f32[16,64,6,128]{3,2,1,0:T(8,128)} %reshape.92, f32[128]{0:T(128)S(1)} %convert_element_type.62, f32[16,64,6]{2,1,0:T(8,128)S(1)} %copy.17), kind=kLoop, calls=%fused_computation.9 | loop fusion | flops 1572864 | bytes 6316544 | tf_op jit(solution)/shard_map/mul | solution.py:23
  48.8 1.9 subtract_convert_fusion
  50.7 2.7 %pad_maximum_fusion = bf16[16,64,6,128]{3,2,1,0:T(8,128)(2,1)} fusion(bf16[16,64,6,64]{3,2,1,0:T(8,128)(2,1)S(1)} %get-tuple-element.4, bf16[16,64,6,64]{3,2,1,0:T(8,128)(2,1)S(1)} %get-tuple-element.3), kind=kLoop, calls=%fused_computation.13 | loop fusion | flops 3145728 | bytes 3145728 | tf_op jit(solution)/shard_map/concatenate | solution.py:34
  53.4 3.5 %convert_element_type.64.q_ref = bf16[16,64,768]{2,1,0:T(8,128)(2,1)S(1)} reshape(bf16[16,64,6,128]{3,2,1,0:T(8,128)(2,1)} %pad_maximum_fusion) | data formatting | bytes 3145728 | tf_op jit(solution)/shard_map/convert_element_type | solution.py:48
  56.9 48.3 %attend.1 = f32[16,200,256]{2,1,0:T(8,128)S(1)} custom-call(s32[16]{0:T(128)S(1)} %copy-done.3, bf16[16,64,768]{2,1,0:T(8,128)(2,1)S(1)} %convert_element_type.64.q_ref, bf16[16,64,256]{2,1,0:T(8,128)(2,1)S(1)} %convert_element_type.70.kn_ref, bf16[16,64,256]{2,1,0:T(8,128)(2,1)S(1)} %fusion.32.vn_ref, bf16[16,4096,128]{2,1,0:T(8,128)(2,1)} %bitcast.23, ...), custom_call_target="tpu_custom_call" | custom-call | tf_op jit(solution)/shard_map/attend/pallas_call | solution.py:163
  105.3 1.7 copy-done.2
  107.0 84.9 %exchange.1 = bf16[16,64,3072]{2,1,0:T(8,128)(2,1)} custom-call(f32[2,2,4,200,256]{4,3,2,1,0:T(8,128)} %bitcast.22, bf16[16,64,3072]{2,1,0:T(8,128)(2,1)} %x_ref.1, bf16[768,3072]{1,0:T(8,128)(2,1)} %wo_ref.1), custom_call_target="tpu_custom_call" | custom-call | tf_op jit(solution)/shard_map/exchange/pallas_call | solution.py:419
  191.9 6.1 %copy.21 = bf16[16,64,3072]{2,1,0:T(8,128)(2,1)} copy(bf16[16,64,3072]{2,1,0:T(8,128)(2,1)} %exchange.1) | data formatting | bytes 12582912
  (15 shorter events, 0.1 us)
Async XLA Ops:
  0.6 7.0 %copy-start = (bf16[3072,256]{1,0:T(8,128)(2,1)S(1)}, bf16[3072,256]{1,0:T(8,128)(2,1)}, u32[]{:S(2)}) copy-start(bf16[3072,256]{1,0:T(8,128)(2,1)} %param.18) | copy-start | bytes 4718596
  0.6 7.0 %copy-start.4 = (bf16[16,64,3072]{2,1,0:T(8,128)(2,1)S(1)}, bf16[16,64,3072]{2,1,0:T(8,128)(2,1)}, u32[]{:S(2)}) copy-start(bf16[16,64,3072]{2,1,0:T(8,128)(2,1)} %x_ref.1) | copy-start | bytes 18874372
  0.7 7.0 %copy-start.6 = (bf16[3072]{0:T(1024)(128)(2,1)S(1)}, bf16[3072]{0:T(1024)(128)(2,1)}, u32[]{:S(2)}) copy-start(bf16[3072]{0:T(1024)(128)(2,1)} %param.15) | copy-start | bytes 18436
  26.6 10.2 %copy-start.5 = (bf16[16,64,2,128]{3,2,1,0:T(2,128)(2,1)}, bf16[16,64,2,128]{3,2,1,0:T(2,128)(2,1)S(1)}, u32[]{:S(2)}) copy-start(bf16[16,64,2,128]{3,2,1,0:T(2,128)(2,1)S(1)} %maximum_convert_fusion) | copy-start | bytes 1572868
  50.7 6.3 %copy-start.3 = (s32[16]{0:T(128)S(1)}, s32[16]{0:T(128)}, u32[]{:S(2)}) copy-start(s32[16]{0:T(128)} %len_ref.1) | copy-start | bytes 196
  105.3 1.7 copy-start.2
  107.0 91.0 %copy-start.1 = (bf16[3072,256]{1,0:T(8,128)(2,1)S(1)}, bf16[3072,256]{1,0:T(8,128)(2,1)}, u32[]{:S(2)}) copy-start(bf16[3072,256]{1,0:T(8,128)(2,1)} %param.18) | copy-start | bytes 4718596

commit v2 on v1

v2 whole, which is shorter than its diff:
```python
import functools

import jax
import jax.numpy as jnp
from jax import lax
from jax.experimental import pallas as pl
from jax.experimental.pallas import tpu as pltpu
from jax.sharding import PartitionSpec as P

HEAD_DIM = 128
MASKED = -1e30
LOW = -3e38
EXP_SCALE = (HEAD_DIM ** -0.5) * 1.4426950408889634
WAVE_SEQS = 4
STAT_ROWS = 8
MESH = pl.DeviceIdType.MESH
F32 = jnp.float32
BF16 = jnp.bfloat16


def rope_tables(prefix_len, n_new):
    half_dim = HEAD_DIM // 2
    positions = prefix_len[:, None] + jnp.arange(n_new, dtype=jnp.int32)[None, :]
    inv_freq = 1.0 / (1000000.0 ** (jnp.arange(half_dim, dtype=F32) * 2.0 / HEAD_DIM))
    angles = positions.astype(F32)[..., None] * inv_freq
    cos_t, sin_t = jnp.cos(angles), jnp.sin(angles)
    return jnp.concatenate([cos_t, cos_t, -sin_t, sin_t], axis=-1).reshape(-1, 2 * HEAD_DIM)


def block_diag(pair):
    zero = jnp.zeros((pair.shape[0], HEAD_DIM), pair.dtype)
    top = jnp.concatenate([pair[:, :HEAD_DIM], zero], axis=1)
    low = jnp.concatenate([zero, pair[:, HEAD_DIM:]], axis=1)
    return jnp.concatenate([top, low], axis=0)


def dot_nt(a, b):
    return lax.dot_general(a, b, (((1,), (1,)), ((), ())), preferred_element_type=F32)


def attend_seq(q_tok, k_ref, v_ref, k_own, v_own, limit, own_on, score_ref, even_ref, odd_ref):
    n_new = q_tok.shape[0]
    n_half = n_new // 2
    group = q_tok.shape[1] // (2 * HEAD_DIM)
    rows = group * n_new
    n_keys = k_ref.shape[0]
    chunk = even_ref.shape[0]
    q_ext = jnp.concatenate([
        jnp.concatenate([q_tok[h * n_half:(h + 1) * n_half, g * HEAD_DIM:(g + 1) * HEAD_DIM],
                         q_tok[h * n_half:(h + 1) * n_half, (group + g) * HEAD_DIM:(group + g + 1) * HEAD_DIM]], axis=1)
        for h in range(2) for g in range(group)], axis=0)
    lane = lax.broadcasted_iota(jnp.int32, (rows, HEAD_DIM), 1)
    is_even = lane % 2 == 0
    key_lane = lax.broadcasted_iota(jnp.int32, (1, chunk), 1)
    run_max = jnp.full((rows, HEAD_DIM), MASKED, F32)
    for start in range(0, n_keys, chunk):
        keys = k_ref[pl.ds(start, chunk), :]
        keys_ext = jnp.concatenate([keys * even_ref[...], keys * odd_ref[...]], axis=1)
        scores = dot_nt(q_ext, keys_ext)
        scores = jnp.where(key_lane < 2 * limit - start, scores, MASKED)
        score_ref[:, pl.ds(start, chunk)] = scores
        for block in range(0, chunk, HEAD_DIM):
            run_max = jnp.maximum(run_max, scores[:, block:block + HEAD_DIM])
    s_own = dot_nt(q_ext, block_diag(k_own))
    row = lax.broadcasted_iota(jnp.int32, (rows, 2 * n_new), 0)
    own_row = jnp.where(row < rows // 2, row, row + n_half) % n_half + jnp.where(row < rows // 2, 0, n_half)
    own_lane = lax.broadcasted_iota(jnp.int32, (rows, 2 * n_new), 1)
    own_first = own_lane < n_new
    own_key = jnp.where(own_first, own_lane, own_lane - n_new)
    s_own = jnp.where((own_key <= own_row) & own_on, s_own, MASKED)
    max_0 = jnp.maximum(jnp.max(jnp.where(is_even, run_max, LOW), axis=1, keepdims=True),
                        jnp.max(jnp.where(own_first, s_own, LOW), axis=1, keepdims=True))
    max_1 = jnp.maximum(jnp.max(jnp.where(is_even, LOW, run_max), axis=1, keepdims=True),
                        jnp.max(jnp.where(own_first, LOW, s_own), axis=1, keepdims=True))
    max_lane = jnp.where(is_even, max_0, max_1)
    p_own = jnp.exp2((s_own - jnp.where(own_first, max_0, max_1)) * EXP_SCALE)
    acc = jnp.dot(p_own.astype(BF16), block_diag(v_own), preferred_element_type=F32)
    run_sum = jnp.zeros((rows, HEAD_DIM), F32)
    for start in range(0, n_keys, chunk):
        probs = []
        for block in range(start, start + chunk, HEAD_DIM):
            p_blk = jnp.exp2((score_ref[:, pl.ds(block, HEAD_DIM)] - max_lane) * EXP_SCALE)
            run_sum = run_sum + p_blk
            probs.append(p_blk.astype(BF16))
        vals = v_ref[pl.ds(start, chunk), :]
        vals_ext = jnp.concatenate([vals * even_ref[...], vals * odd_ref[...]], axis=1)
        acc = acc + jnp.dot(jnp.concatenate(probs, axis=1), vals_ext, preferred_element_type=F32)
    sum_0 = jnp.sum(jnp.where(is_even, run_sum, 0.0) + jnp.where(own_first, p_own, 0.0), axis=1, keepdims=True)
    sum_1 = jnp.sum(jnp.where(is_even, 0.0, run_sum) + jnp.where(own_first, 0.0, p_own), axis=1, keepdims=True)
    stat = jnp.where(lane == 0, max_0, jnp.where(lane == 1, max_1, jnp.where(lane == 2, sum_0, sum_1)))
    pad = jnp.zeros((HEAD_DIM - rows // 2, HEAD_DIM), F32)
    stat = jnp.concatenate([stat[:rows // 2], pad, stat[rows // 2:], pad], axis=0)
    return acc, stat.T[:STAT_ROWS]


def merge_units(units, rows, normalise):
    stats = [u[rows:rows + STAT_ROWS, :HEAD_DIM] for u in units]
    peak = functools.reduce(jnp.maximum, [s[0:2] for s in stats])
    facs = [jnp.exp2((s[0:2] - peak) * EXP_SCALE) for s in stats]
    total = functools.reduce(jnp.add, [s[2:4] * f for s, f in zip(stats, facs)])
    if normalise:
        facs = [f / total for f in facs]
    table = jnp.concatenate(facs, axis=0)
    table = jnp.concatenate([table, jnp.zeros((HEAD_DIM - table.shape[0], table.shape[1]), F32)], axis=0).T
    heads = []
    for h in range(2):
        parts = [u[:rows, h * HEAD_DIM:(h + 1) * HEAD_DIM] * table[:rows, 2 * i + h:2 * i + h + 1] for i, u in enumerate(units)]
        heads.append(functools.reduce(jnp.add, parts))
    stat = jnp.concatenate([peak, total, jnp.zeros((STAT_ROWS - 4, total.shape[1]), F32)], axis=0)
    return jnp.concatenate(heads, axis=1), stat


class Exchange:
    def __init__(self, wave, refs, n_cp, n_tp):
        self.w = wave
        self.r = refs
        self.n_x = n_cp // 2
        self.n_cp = n_cp
        self.n_tp = n_tp
        self.cp = lax.axis_index('cp')
        self.tp = lax.axis_index('tp')
        self.x = self.cp // 2
        self.core = self.cp % 2

    def cp_at(self, dx):
        return lax.rem(self.cp + 2 * dx + self.n_cp, self.n_cp)

    def tp_at(self, dy):
        return lax.rem(self.tp + dy + self.n_tp, self.n_tp)

    def send(self, src, dst, recv_sem, cp=None, tp=None):
        where = {}
        if cp is not None:
            where['cp'] = cp
        if tp is not None:
            where['tp'] = tp
        sent = self.r['sent']
        copy = pltpu.make_async_remote_copy(src_ref=src, dst_ref=dst, send_sem=self.r['send'].at[self.w, len(sent)], recv_sem=recv_sem,
                                            device_id=where, device_id_type=MESH)
        copy.start()
        sent.append(src.shape)

    def wait(self, dst, recv_sem):
        pltpu.make_async_remote_copy(src_ref=dst, dst_ref=dst, send_sem=self.r['send'].at[0, 0], recv_sem=recv_sem,
                                     device_id={'cp': self.cp}, device_id_type=MESH).wait_recv()

    def wait_sends(self):
        for k, shape in enumerate(self.r['sent']):
            name = 'pair' if len(shape) == 3 else 'xin' if shape[0] == self.r['pair'].shape[2] else 'gather'
            ref = {'pair': lambda: self.r['pair'].at[self.w], 'xin': lambda: self.r['xin'].at[self.w, 0],
                   'gather': lambda: self.r['gather'].at[self.w, 0, 0, pl.ds(0, shape[0]), :]}[name]()
            pltpu.make_async_remote_copy(src_ref=ref, dst_ref=ref, send_sem=self.r['send'].at[self.w, k], recv_sem=self.r['pair_sem'].at[0],
                                         device_id={'cp': self.cp}, device_id_type=MESH).wait_send()

    @property
    def partner(self):
        return self.cp + 1 - 2 * self.core

    def pair_send(self):
        r, w = self.r, self.w
        self.send(r['sums'].at[w, 1 - self.core], r['pair'].at[w], r['pair_sem'].at[w], cp=self.partner)

    def pair_merge(self):
        r, w, rows = self.r, self.w, self.r['rows']
        self.wait(r['pair'].at[w], r['pair_sem'].at[w])
        for d in (2, 1, 3, 0):
            ox = lax.rem(self.x + d, self.n_x)
            merged, stat = merge_units([r['pair'][w, ox], r['sums'][w, self.core, ox]], rows, False)
            r['pair'][w, ox, pl.ds(0, rows), :] = merged
            r['pair'][w, ox, pl.ds(rows, STAT_ROWS), pl.ds(0, HEAD_DIM)] = stat
            if d:
                self.send(r['pair'].at[w, ox], r['xin'].at[w, d - 1], r['xin_sem'].at[w, d - 1], cp=self.cp_at(d))

    def project_out(self):
        r, w, rows = self.r, self.w, self.r['rows']
        for d in range(1, self.n_x):
            self.wait(r['xin'].at[w, d - 1], r['xin_sem'].at[w, d - 1])
        units = [r['pair'][w, self.x]] + [r['xin'][w, d - 1] for d in range(1, self.n_x)]
        attn, _ = merge_units(units, rows, True)
        attn = attn.astype(BF16)
        n_half = r['n_half']
        group = rows // n_half
        lhs = jnp.concatenate([attn[g * n_half:(g + 1) * n_half, k * HEAD_DIM:(k + 1) * HEAD_DIM] for k in range(2) for g in range(group)], axis=1)
        width = r['wo'].shape[1] // self.n_tp
        for d in (2, 1, 3, 0):
            oy = lax.rem(self.tp + d, self.n_tp)
            for part in range(0, width, 256):
                cols = pl.ds(pl.multiple_of(oy * width + part, 128), 256)
                r['yout'][w, oy, :, pl.ds(part, 256)] = jnp.dot(lhs, r['wo'][:, cols], preferred_element_type=F32)
            if d:
                self.send(r['yout'].at[w, oy], r['yin'].at[w, d - 1], r['yin_sem'].at[w, d - 1], tp=self.tp_at(d))

    def finish_rows(self):
        r, w = self.r, self.w
        for d in range(1, self.n_tp):
            self.wait(r['yin'].at[w, d - 1], r['yin_sem'].at[w, d - 1])
        width = r['wo'].shape[1] // self.n_tp
        n_half = r['n_half']
        total = r['yout'][w, self.tp]
        for d in range(1, self.n_tp):
            total = total + r['yin'][w, d - 1]
        row = pl.multiple_of((w * self.n_cp + self.cp) * n_half, n_half)
        cols = pl.ds(pl.multiple_of(self.tp * width, 128), width)
        total = total + r['x'][pl.ds(row, n_half), cols].astype(F32)
        r['gather'][w, self.cp, self.tp] = total.astype(BF16).astype(F32)

    def unit(self, half, rx, ry, sub=None):
        size = self.r['n_half'] // 2
        start = half * size
        if sub is not None:
            start, size = start + sub * (size // 2), size // 2
        return self.r['gather'].at[self.w, self.cp_at(rx), self.tp_at(ry), pl.ds(start, size), :]

    def hop(self, half, rx, ry, axis, step, sub=None):
        ref = self.unit(half, rx, ry, sub)
        tx, ty = (rx - step) % self.n_x, ry
        if axis == 'y':
            tx, ty = rx, (ry - step) % self.n_tp
        sem = self.r['gather_sem'].at[self.w, half, tx, ty, sub or 0]
        if axis == 'x':
            self.send(ref, ref, sem, cp=self.cp_at(step))
        else:
            self.send(ref, ref, sem, tp=self.tp_at(step))

    def arrive(self, half, rx, ry, sub=None):
        self.wait(self.unit(half, rx, ry, sub), self.r['gather_sem'].at[self.w, half, rx, ry, sub or 0])

    def share(self, half, rx, ry):
        ref = self.unit(half, rx, ry)
        self.send(ref, ref, self.r['share_sem'].at[self.w, half, rx, ry], cp=self.partner)

    def axes(self, half):
        return ('x', 'y') if half == 0 else ('y', 'x')

    def at(self, half, a, b):
        return (a, b) if half == 0 else (b, a)

    def gather_start(self):
        for half in (0, 1):
            for axis in self.axes(half):
                for step in (1, -1):
                    self.hop(half, 0, 0, axis, step)
        for half in (0, 1):
            self.share(half, 0, 0)

    def gather_first(self):
        for a, step in ((3, 1), (1, -1)):
            for half in (0, 1):
                one, two = self.axes(half)
                rx, ry = self.at(half, a, 0)
                self.arrive(half, rx, ry)
                self.hop(half, rx, ry, one, step, sub=0 if step == 1 else 1)
                self.hop(half, rx, ry, two, 1)
                self.hop(half, rx, ry, two, -1)
                self.share(half, rx, ry)

    def gather_opposite(self):
        for half in (0, 1):
            one, two = self.axes(half)
            rx, ry = self.at(half, 2, 0)
            self.arrive(half, rx, ry, 0)
            self.arrive(half, rx, ry, 1)
            self.hop(half, rx, ry, two, 1)
            self.hop(half, rx, ry, two, -1)
            self.share(half, rx, ry)

    def gather_second(self):
        for a in (0, 3, 1, 2):
            for b, step in ((3, 1), (1, -1)):
                for half in (0, 1):
                    one, two = self.axes(half)
                    rx, ry = self.at(half, a, b)
                    self.arrive(half, rx, ry)
                    self.hop(half, rx, ry, two, step, sub=0 if step == 1 else 1)
                    self.share(half, rx, ry)

    def gather_last(self):
        for a in (0, 3, 1, 2):
            for half in (0, 1):
                rx, ry = self.at(half, a, 2)
                self.arrive(half, rx, ry, 0)
                self.arrive(half, rx, ry, 1)
                self.share(half, rx, ry)

    def gather_shared(self):
        size = self.r['n_half'] // 2
        for half in (0, 1):
            for rx in range(self.n_x):
                for ry in range(self.n_tp):
                    cp = self.cp_at(rx) + 1 - 2 * self.core
                    ref = self.r['gather'].at[self.w, cp, self.tp_at(ry), pl.ds(half * size, size), :]
                    self.wait(ref, self.r['share_sem'].at[self.w, half, rx, ry])

    def out_copy(self, w):
        r = self.r
        n_rows = r['stage'].shape[1]
        return pltpu.make_async_copy(r['stage'].at[w % 2], r['out'].at[pl.ds(pl.multiple_of(w * n_rows, n_rows), n_rows), :], r['out_sem'].at[w % 2])

    def write_rows(self):
        r, w = self.r, self.w
        n_half = r['n_half']
        width = r['wo'].shape[1] // self.n_tp

        @pl.when(w >= 2)
        def _():
            self.out_copy(w - 2).wait()

        def body(s, carry):
            row = pl.ds(pl.multiple_of(s * n_half, n_half), n_half)
            for ty in range(self.n_tp):
                r['stage'][w % 2, row, pl.ds(ty * width, width)] = r['gather'][w, s, ty].astype(BF16)
            return carry
        lax.fori_loop(0, self.n_cp, body, 0)
        self.out_copy(w).start()


def entry_barrier(n_cp, n_tp):
    cp, tp = lax.axis_index('cp'), lax.axis_index('tp')
    barrier = pltpu.get_barrier_semaphore()
    peers = [{'cp': cp + 1 - 2 * (cp % 2)}]
    peers += [{'cp': lax.rem(cp + 2 * d, n_cp)} for d in range(1, n_cp // 2)]
    peers += [{'tp': lax.rem(tp + d, n_tp)} for d in range(1, n_tp)]
    for peer in peers:
        pl.semaphore_signal(barrier, inc=1, device_id=peer, device_id_type=MESH)
    pl.semaphore_wait(barrier, len(peers))


def project_block(block, r):
    n_rows = r['normed'].shape[0]
    base = pl.multiple_of(block * n_rows, n_rows)

    def norm_rows(t, carry):
        step = 32
        row = pl.multiple_of(t * step, step)
        x = r['x'][pl.ds(base + row, step), :].astype(F32)
        scale = lax.rsqrt(jnp.mean(jnp.square(x), axis=1, keepdims=True) + 1e-6)
        r['normed'][pl.ds(row, step), :] = (x * scale * r['gain'][...]).astype(BF16)
        return carry
    lax.fori_loop(0, n_rows // 32, norm_rows, 0)
    cos_t = r['rope'][pl.ds(base, n_rows), :HEAD_DIM]
    sin_t = r['rope'][pl.ds(base, n_rows), HEAD_DIM:]
    n_q = r['q'].shape[1] // HEAD_DIM

    def rotate(lin, gain):
        lin = lin.astype(BF16).astype(F32)
        lin = lin * lax.rsqrt(jnp.mean(jnp.square(lin), axis=1, keepdims=True) + 1e-6) * gain
        return lin * cos_t + pltpu.roll(lin, HEAD_DIM // 2, 1) * sin_t
    for pair in range(n_q // 2 + 2):
        lin = jnp.dot(r['normed'][...], r['w'][:, pl.ds(pair * 2 * HEAD_DIM, 2 * HEAD_DIM)], preferred_element_type=F32)
        for h in range(2):
            part = lin[:, h * HEAD_DIM:(h + 1) * HEAD_DIM]
            lanes = pl.ds(h * HEAD_DIM, HEAD_DIM)
            if pair < n_q // 2:
                r['q'][:, pl.ds((2 * pair + h) * HEAD_DIM, HEAD_DIM)] = rotate(part, r['q_norm'][...]).astype(BF16)
                continue
            name = 'k' if pair == n_q // 2 else 'v'
            part = rotate(part, r['k_norm'][...]) if name == 'k' else part
            part = part.astype(BF16)
            r[name][:, lanes] = part
            r['mix'][pl.ds(h, n_rows, stride=2), :] = part.astype(F32)
        if pair >= n_q // 2:
            name = 'k' if pair == n_q // 2 else 'v'
            rows = pl.ds(pl.multiple_of(2 * base, 2 * n_rows), 2 * n_rows)
            r[name + '_stage'][rows, :] = r['mix'][...].astype(BF16)
            pltpu.make_async_copy(r[name + '_stage'].at[rows, :], r[name + '_out'].at[rows, :], r['new_sem'].at[block, 0 if name == 'k' else 1]).start()


PHASES = (('pair_send', 3), ('pair_merge', 4), ('project_out', 6), ('finish_rows+gather_start', 8), ('gather_first', 9), ('gather_opposite', 10),
          ('gather_second', 12), ('gather_last', 14), ('gather_shared+write_rows', 15))


def block_kernel(n_cp, n_tp, len_ref, rope_hbm, gain_ref, qn_ref, kn_ref, x_hbm, wq_hbm, wk_hbm, wv_hbm, wo_hbm, k_hbm, v_hbm,
                 out_ref, kout_ref, vout_ref,
                 x_buf, w_buf, wo_buf, rope_buf, normed, q_buf, k_new, v_new, mix, k_stage, v_stage, k_buf, v_buf, score, even, odd,
                 sums, pair, xin, yout, yin, gather, stage,
                 load_sem, x_sem, k_sem, v_sem, new_sem, send_sem, pair_sem, xin_sem, yin_sem, gather_sem, share_sem, out_sem):
    n_seq, n_keys = k_hbm.shape[0], k_hbm.shape[1]
    n_waves = n_seq // WAVE_SEQS
    n_new = x_buf.shape[0] // n_seq
    wave_rows = WAVE_SEQS * n_new
    cp_index = lax.axis_index('cp')

    def kv_copies(i, slot):
        return (pltpu.make_async_copy(k_hbm.at[i], k_buf.at[slot], k_sem.at[slot]),
                pltpu.make_async_copy(v_hbm.at[i], v_buf.at[slot], v_sem.at[slot]))

    def x_copy(b):
        rows = pl.ds(b * wave_rows, wave_rows)
        return pltpu.make_async_copy(x_hbm.at[rows, :], x_buf.at[rows, :], x_sem.at[b])
    q_width, kv_width = wq_hbm.shape[1], wk_hbm.shape[1]
    loads = [pltpu.make_async_copy(rope_hbm, rope_buf, load_sem.at[0]),
             pltpu.make_async_copy(wq_hbm, w_buf.at[:, pl.ds(0, q_width)], load_sem.at[1]),
             pltpu.make_async_copy(wk_hbm, w_buf.at[:, pl.ds(q_width, kv_width)], load_sem.at[2]),
             pltpu.make_async_copy(wv_hbm, w_buf.at[:, pl.ds(q_width + kv_width, kv_width)], load_sem.at[3])]
    x_copy(0).start()
    for load in loads:
        load.start()
    for copy in kv_copies(0, 0):
        copy.start()
    for b in range(1, n_waves):
        x_copy(b).start()
    wo_load = pltpu.make_async_copy(wo_hbm, wo_buf, load_sem.at[4])
    wo_load.start()
    entry_barrier(n_cp, n_tp)
    parity = (lax.broadcasted_iota(jnp.int32, even.shape, 0) % 2).astype(F32)
    odd[...] = parity.astype(BF16)
    even[...] = (1.0 - parity).astype(BF16)
    for b in range(n_waves):
        if b == 0:
            x_copy(b).wait()
    for load in loads:
        load.wait()
    refs = {'x': x_buf, 'w': w_buf, 'wo': wo_buf, 'rope': rope_buf, 'gain': gain_ref, 'q_norm': qn_ref, 'k_norm': kn_ref, 'normed': normed,
            'q': q_buf, 'k': k_new, 'v': v_new, 'mix': mix, 'k_stage': k_stage, 'v_stage': v_stage, 'k_out': kout_ref, 'v_out': vout_ref,
            'new_sem': new_sem, 'sums': sums, 'pair': pair, 'xin': xin, 'yout': yout, 'yin': yin, 'gather': gather, 'stage': stage, 'out': out_ref,
            'send': send_sem, 'pair_sem': pair_sem, 'xin_sem': xin_sem, 'yin_sem': yin_sem, 'gather_sem': gather_sem, 'share_sem': share_sem,
            'out_sem': out_sem, 'rows': pair.shape[2] - STAT_ROWS, 'n_half': n_new // 2, 'sent': []}
    rows = refs['rows']

    def attention(i):
        wave, j, slot = i // WAVE_SEQS, i % WAVE_SEQS, i % 2

        @pl.when(i + 1 < n_seq)
        def _():
            for copy in kv_copies(i + 1, 1 - slot):
                copy.start()
        for copy in kv_copies(i, slot):
            copy.wait()
        limit = len_ref[i] - cp_index * (n_keys // 2)
        toks = pl.ds(pl.multiple_of(j * n_new, n_new), n_new)
        acc, stat = attend_seq(q_buf[toks, :], k_buf.at[slot], v_buf.at[slot], k_new[toks, :], v_new[toks, :], limit, cp_index == 0, score, even, odd)
        for h in range(2):
            sums[wave, h, j, pl.ds(0, rows), :] = acc[h * rows:(h + 1) * rows]
            sums[wave, h, j, pl.ds(rows, STAT_ROWS), pl.ds(0, HEAD_DIM)] = stat[:, h * HEAD_DIM:(h + 1) * HEAD_DIM]

    def step(i, carry):
        refs['sent'] = []

        @pl.when((i < n_seq) & (i % WAVE_SEQS == 0))
        def _():
            block = i // WAVE_SEQS

            @pl.when(block > 0)
            def _():
                rows_b = pl.ds(pl.multiple_of(block * wave_rows, wave_rows), wave_rows)
                pltpu.make_async_copy(x_hbm.at[rows_b, :], x_buf.at[rows_b, :], x_sem.at[block]).wait()
            project_block(block, refs)

        @pl.when(i < n_seq)
        def _():
            attention(i)

        @pl.when(i == WAVE_SEQS)
        def _():
            wo_load.wait()
        for name, delay in PHASES:
            at = i - delay

            @pl.when((at >= 0) & (at % WAVE_SEQS == 0) & (at < n_seq))
            def _(name=name, at=at):
                wave = Exchange(at // WAVE_SEQS, refs, n_cp, n_tp)
                for part in name.split('+'):
                    getattr(wave, part)()
        return carry
    lax.fori_loop(0, n_seq - WAVE_SEQS + PHASES[-1][1] + 1, step, 0)

    def drain(w, carry):
        wave = Exchange(w, refs, n_cp, n_tp)
        wave.wait_sends()
        rows_w = pl.ds(pl.multiple_of(2 * w * wave_rows, 2 * wave_rows), 2 * wave_rows)
        pltpu.make_async_copy(k_stage.at[rows_w, :], kout_ref.at[rows_w, :], new_sem.at[w, 0]).wait()
        pltpu.make_async_copy(v_stage.at[rows_w, :], vout_ref.at[rows_w, :], new_sem.at[w, 1]).wait()

        @pl.when(w >= n_waves - 2)
        def _():
            wave.out_copy(w).wait()
        return carry
    lax.fori_loop(0, n_waves, drain, 0)


def solution(mesh):
    n_cp, n_tp = mesh.shape['cp'], mesh.shape['tp']

    def per_device(hidden, prefix_len, k_cache, v_cache, attn_norm, w_q, w_k, w_v, w_o, q_norm, k_norm):
        n_seq, n_new, d_model = hidden.shape
        n_keys = k_cache.shape[1] * 2
        n_waves, n_x, n_half = n_seq // WAVE_SEQS, n_cp // 2, n_new // 2
        wave_rows = WAVE_SEQS * n_new
        q_width, kv_width = w_q.shape[1], w_k.shape[1]
        rows = n_half * q_width // (2 * HEAD_DIM)
        unit = (rows + STAT_ROWS, 2 * HEAD_DIM)
        width = d_model // n_tp
        chunk = min(512, n_keys)
        n_send = 1 + (n_x - 1) + (n_tp - 1) + 40 + 32
        vmem = pl.BlockSpec(memory_space=pltpu.VMEM)
        hbm = pl.BlockSpec(memory_space=pl.ANY)
        dma = pltpu.SemaphoreType.DMA
        block_out, k_new, v_new = pl.pallas_call(
            functools.partial(block_kernel, n_cp, n_tp),
            out_shape=(jax.ShapeDtypeStruct((n_seq * n_new, d_model), BF16), jax.ShapeDtypeStruct((n_seq * n_new * 2, HEAD_DIM), BF16),
                       jax.ShapeDtypeStruct((n_seq * n_new * 2, HEAD_DIM), BF16)),
            in_specs=[pl.BlockSpec(memory_space=pltpu.SMEM), hbm, vmem, vmem, vmem] + [hbm] * 7,
            out_specs=(hbm, hbm, hbm),
            scratch_shapes=[
                pltpu.VMEM((n_seq * n_new, d_model), BF16),
                pltpu.VMEM((d_model, q_width + 2 * kv_width), BF16),
                pltpu.VMEM((q_width, d_model), BF16),
                pltpu.VMEM((n_seq * n_new, 2 * HEAD_DIM), F32),
                pltpu.VMEM((wave_rows, d_model), BF16),
                pltpu.VMEM((wave_rows, q_width), BF16),
                pltpu.VMEM((wave_rows, kv_width), BF16),
                pltpu.VMEM((wave_rows, kv_width), BF16),
                pltpu.VMEM((2 * wave_rows, HEAD_DIM), F32),
                pltpu.VMEM((2 * n_seq * n_new, HEAD_DIM), BF16),
                pltpu.VMEM((2 * n_seq * n_new, HEAD_DIM), BF16),
                pltpu.VMEM((2, n_keys, HEAD_DIM), BF16),
                pltpu.VMEM((2, n_keys, HEAD_DIM), BF16),
                pltpu.VMEM((2 * rows, n_keys), F32),
                pltpu.VMEM((chunk, HEAD_DIM), BF16),
                pltpu.VMEM((chunk, HEAD_DIM), BF16),
                pltpu.VMEM((n_waves, 2, n_x) + unit, F32),
                pltpu.VMEM((n_waves, n_x) + unit, F32),
                pltpu.VMEM((n_waves, n_x - 1) + unit, F32),
                pltpu.VMEM((n_waves, n_tp, n_half, width), F32),
                pltpu.VMEM((n_waves, n_tp - 1, n_half, width), F32),
                pltpu.VMEM((n_waves, n_cp, n_tp, n_half, width), F32),
                pltpu.VMEM((2, wave_rows, d_model), BF16),
                dma((5,)), dma((n_waves,)), dma((2,)), dma((2,)), dma((n_waves, 2)), dma((n_waves, n_send)), dma((n_waves,)),
                dma((n_waves, n_x - 1)), dma((n_waves, n_tp - 1)), dma((n_waves, 2, n_x, n_tp, 2)), dma((n_waves, 2, n_x, n_tp)), dma((2,)),
            ],
            compiler_params=pltpu.CompilerParams(collective_id=0, has_side_effects=True, vmem_limit_bytes=67043328),
            name='block',
        )(prefix_len, rope_tables(prefix_len, n_new), attn_norm.astype(F32)[None], q_norm.astype(F32)[None], k_norm.astype(F32)[None],
          hidden.reshape(n_seq * n_new, d_model), w_q, w_k, w_v, w_o,
          k_cache.reshape(n_seq, n_keys, HEAD_DIM), v_cache.reshape(n_seq, n_keys, HEAD_DIM))
        new_shape = (n_seq, n_new, 2, HEAD_DIM)
        return block_out.reshape(n_seq, n_new, d_model), k_new.reshape(new_shape), v_new.reshape(new_shape)

    cache_spec = P('dp', 'cp', 'tp', None)
    arg_specs = (P('dp', None, None), P('dp'), cache_spec, cache_spec, P(None), P(None, 'tp'), P(None, 'tp'), P(None, 'tp'), P('tp', None), P(None), P(None))
    out_specs = (P('dp', None, None), P('dp', None, 'tp', None), P('dp', None, 'tp', None))
    return jax.shard_map(per_device, mesh=mesh, in_specs=arg_specs, out_specs=out_specs, check_vma=False)
```

time: 198 us -> 150 us (0.76)
  other arithmetic: 26.4 us -> 6.59 us
  matrix products: 17.7 us -> 0 us
  local copies, waits for them, and re-layouts: 19.8 us -> 7.85 us
  Pallas kernels: 133 us -> 135 us
    dot_general x3 -> x0, matrix products: 17.7 us -> none  [the longest x1 9.82 us: project_new(): jnp.einsum('bce,ef->bcf', normed, w_q, preferred_element_type=F32)]
    convert_element_type x4 -> x1, local copies, waits for them, and re-layouts: 10.2 us -> 0.07 us  [rope_tables(): angles = positions.astype(F32)[..., None] * inv_freq]
    reduce_sum x3 -> x0, other arithmetic: 8.6 us -> none  [rms_scale(): mean_sq = jnp.mean(jnp.square(tensor), axis=-1, keepdims=True)]
    mul x2 -> x0, other arithmetic: 5.16 us -> none  [rms_scale(): return tensor * lax.rsqrt(mean_sq + 1e-06) * norm_gain]
    convert_element_type x5 -> x1, other arithmetic: 4.3 us -> 0.73 us  [rope_tables(): angles = positions.astype(F32)[..., None] * inv_freq]
    broadcast_in_dim x0 -> x2, other arithmetic: none -> 2.51 us  [the longest x1 1.29 us: per_device(): attn_norm.astype(F32)[None]]
    pallas_call x2 -> x1, Pallas kernels: 133 us -> 135 us  [per_device(): pl.pallas_call(functools.partial(block_kernel, n_cp, n_tp), out_shape=(ja...]
    unnamed x15 -> x7, local copies, waits for them, and re-layouts: 7.84 us -> 7.78 us
where the time goes in v2:
time: 150 us
  Pallas kernels  135 us (90%)
  local copies, waits for them, and re-layouts  7.85 us (5%)
  other arithmetic  6.59 us (4%)
    pallas_call x1, Pallas kernels, per_device(): pl.pallas_call(functools.partial(block_kernel, n_cp, n_tp), out_shape=(ja...  135 us
    unnamed x7, local copies, waits for them, and re-layouts  7.78 us

profile of v2, /device:TPU:97, one launch (start us, length us, event | category | flops | bytes accessed | tf_op | source)
XLA Modules:
  0.0 149.6 jit_solution(18439907095491063983)
XLA Ops:
  0.6 1.2 bitcast_convert_fusion
  1.9 0.7 add_convert_fusion
  2.6 0.1 convert_element_type.14
  2.7 1.3 broadcast_in_dim.25
  4.0 1.9 %multiply_cosine_fusion = (f32[1024,64]{1,0:T(8,128)S(1)}, f32[1024,64]{1,0:T(8,128)S(1)}, f32[1024,64]{1,0:T(8,128)S(1)}) fusion(f32[1024]{0:T(1024)S(1)} %convert_element_type.14, f32[64]{0:T(128)S(1)} %negate_power_fusion), kind=kLoop, calls=%fused_computation.2 | loop fusion | flops 131072 | bytes 790784 | tf_op jit(solution)/shard_map/cos | solution.py:26
  5.9 1.4 pad_maximum_fusion.rope_hbm
  7.3 134.5 %block.1 = (bf16[1024,3072]{1,0:T(8,128)(2,1)}, bf16[2048,128]{1,0:T(8,128)(2,1)}, bf16[2048,128]{1,0:T(8,128)(2,1)}) custom-call(s32[16]{0:T(128)} %len_ref.1, f32[1024,256]{1,0:T(8,128)} %pad_maximum_fusion.rope_hbm, f32[1,3072]{1,0:T(1,128)} %bitcast.19, f32[1,128]{1,0:T(1,128)} %get-tuple-element.13.qn_ref, f32[1,128]{1,0:T(1,128)} %get-tuple-element.12.kn_ref, ...), custom_call_target="tpu_custom_call" | custom-call | tf_op jit(solution)/shard_map/block/pallas_call | solution.py:498
  141.8 0.0 copy-start.1
  141.9 0.0 copy-start
  141.9 6.2 %copy.18 = bf16[16,64,3072]{2,1,0:T(8,128)(2,1)} copy(bf16[16,64,3072]{2,1,0:T(8,128)(2,1)} %bitcast.15) | data formatting | bytes 12582912
  148.0 0.0 copy-done.1
  148.0 0.8 copy.19
  148.8 0.0 copy-done
  148.8 0.8 copy.20
  (1 shorter events, 0.0 us)
Async XLA Ops:
  141.8 6.2 %copy-start.1 = (bf16[2048,128]{1,0:T(8,128)(2,1)S(1)}, bf16[2048,128]{1,0:T(8,128)(2,1)}, u32[]{:S(2)}) copy-start(bf16[2048,128]{1,0:T(8,128)(2,1)} %get-tuple-element.7) | copy-start | bytes 1572868
  141.9 7.0 %copy-start = (bf16[2048,128]{1,0:T(8,128)(2,1)S(1)}, bf16[2048,128]{1,0:T(8,128)(2,1)}, u32[]{:S(2)}) copy-start(bf16[2048,128]{1,0:T(8,128)(2,1)} %get-tuple-element.8) | copy-start | bytes 1572868
